TPU v7x, 512 devices: a whole 4x8x8 slice. The times are simulated.
512 devices in a mesh: grid: 64 (over y, z), freq: 8 (over x, core).
Axes of the slice: x: 4, y: 8, z: 8, core: 2. Of those that a mesh axis runs over, the one named last changes fastest.
Arguments:
- replicas: bfloat16 [16, 32768, 2, 512], P('freq', 'grid'), may hold values from -6 to 6
- csm: bfloat16 [16, 2, 512, 512], P('freq', None, 'grid'), as said below
- inverse: bfloat16 [16, 2, 512, 512], P('freq', None, 'grid'), as said below
Outputs:
- bartlett: float32 [32768], P(('grid', 'freq'))
- mvdr: float32 [32768], P(('grid', 'freq'))
Inputs may be any that keep to these rules, and one draw needn't show every extreme that they name: csm[f, 0] + i csm[f, 1] is Hermitian positive definite for every bin. inverse[f, 0] + i inverse[f, 1] is Hermitian positive definite for every bin.
All inputs are finite; a program needn't handle non-finite values.
Results may differ from a plain program's by a relative error of at most 0.0003.
Values may be sent and summed in bfloat16 or wider, within the bound.
No kernel may reach another device: no remote copies, remote signals or barrier semaphores. Data moves between devices by JAX's collectives and lax.ppermute only.
A program may use at most 64 MiB of HBM per device.

v0:
```python
import functools

import jax
import jax.numpy as jnp
import numpy as np
from jax import lax
from jax.experimental import pallas as pl
from jax.experimental.layout import Layout, with_layout_constraint
from jax.experimental.pallas import tpu as pltpu
from jax.sharding import Mesh
from jax.sharding import PartitionSpec as P

ALL = ("yh", "yl", "zh", "zl", "x", "c")
MIB = 1 << 20


def device_ids(shape):
    return np.arange(np.prod(shape)).reshape(shape)


def lines(shape, first):
    ids = device_ids(shape)
    by_y = np.moveaxis(ids, 0, -1)
    by_z = np.moveaxis(ids, 1, -1)
    pair = (by_z, by_y) if first else (by_y, by_z)
    picked = [part[..., core, :].reshape(-1, part.shape[-1]) for core, part in enumerate(pair)]
    return np.concatenate(picked, axis=0).tolist()


def partners(shape):
    ids = device_ids(shape)
    pairs = []
    for core in range(shape[3]):
        plane = ids[..., core]
        other = plane[np.arange(shape[0]) ^ 1] if core == 0 else plane[:, np.arange(shape[1]) ^ 1]
        pairs += zip(plane.ravel().tolist(), other.ravel().tolist())
    return pairs


def role():
    return jnp.where(lax.axis_index("c") == 0, lax.axis_index("yl"), lax.axis_index("zl"))


def pack_kernel(n_z, csm_hbm, inverse_hbm, held_hbm, rows_hbm, given_hbm, matrices, packed, room, sems):
    bins, _, depth, width = csm_hbm.shape
    to_all, (parts, size) = rows_hbm.shape[0], room.shape[:2]
    chosen = 1 - role()
    reads = [pltpu.make_async_copy(ref, matrices.at[k], sems.at[k]) for k, ref in enumerate((csm_hbm, inverse_hbm))]
    at = len(reads)
    takes = [
        pltpu.make_async_copy(held_hbm.at[chosen, pl.ds(k * size, size)], room.at[k], sems.at[at + k])
        for k in range(parts)
    ]
    at += parts
    gives = [
        pltpu.make_async_copy(room.at[k], given_hbm.at[pl.ds(k * size, size)], sems.at[at + k]) for k in range(parts)
    ]
    at += parts
    sends = [pltpu.make_async_copy(packed, rows_hbm.at[to], sems.at[at + to]) for to in range(to_all)]
    for copy in reads + takes:
        copy.start()
    y = lax.axis_index("yh") * 2 + lax.axis_index("yl")
    z = lax.axis_index("zh") * 2 + lax.axis_index("zl")
    start = (y * n_z + z) * depth
    row = start + lax.broadcasted_iota(jnp.int32, (depth, width), 0)
    col = lax.broadcasted_iota(jnp.int32, (depth, width), 1)
    weight = jnp.where(col == row, 0.5, 1.0)
    for copy in reads:
        copy.wait()
    for b in range(bins):
        for m in range(2):
            real = matrices[m, b, 0].astype(jnp.float32) * weight
            imag = matrices[m, b, 1].astype(jnp.float32)
            packed[b, m] = jnp.where(col >= row, real, imag).astype(packed.dtype)
    for take, give in zip(takes, gives):
        take.wait()
        give.start()
    for copy in sends:
        copy.start()
    for copy in sends + gives:
        copy.wait()


def pack(n_z, csm, inverse, held, parts=4):
    bins, _, depth, width = csm.shape
    _, points, two, _ = held.shape
    hbm = pl.BlockSpec(memory_space=pltpu.HBM)
    return pl.pallas_call(
        functools.partial(pack_kernel, n_z),
        out_shape=(
            jax.ShapeDtypeStruct((n_z, bins, 2, depth, width), csm.dtype),
            jax.ShapeDtypeStruct(held.shape[1:], held.dtype),
        ),
        in_specs=[hbm] * 3,
        out_specs=[hbm] * 2,
        scratch_shapes=[
            pltpu.VMEM((2, *csm.shape), csm.dtype),
            pltpu.VMEM((bins, 2, depth, width), csm.dtype),
            pltpu.VMEM((parts, points // parts, two, width), held.dtype),
            pltpu.SemaphoreType.DMA((2 + 2 * parts + n_z,)),
        ],
        cost_estimate=pl.CostEstimate(flops=0, bytes_accessed=2 * held.size, transcendentals=0),
        compiler_params=pltpu.CompilerParams(vmem_limit_bytes=61 * MIB),
        name="pack",
    )(csm, inverse, held)


def forms_kernel(rows_ref, own_ref, other_ref, e_own_ref, e_other_ref, out_ref, mat_ref):
    n_y, n_z, _, depth, width = rows_ref.shape
    half = width // 2
    core = lax.axis_index("c")
    swapped = core == 1

    for m in range(2):
        for at in range(n_y * n_z):
            y, z = at // n_z, at % n_z
            first, second = jnp.where(swapped, z, y), jnp.where(swapped, y, z)
            mat_ref[m, at * depth : (at + 1) * depth, :] = rows_ref[first, second, m]
    row = lax.broadcasted_iota(jnp.int32, (half, half), 0)
    col = lax.broadcasted_iota(jnp.int32, (half, half), 1)
    upper = col >= row
    zero = jnp.zeros((half, half), mat_ref.dtype)
    dot = functools.partial(jnp.dot, preferred_element_type=jnp.float32)
    lanes = lambda *parts: jnp.concatenate(parts, axis=1)
    tall = lambda *parts: jnp.concatenate(parts, axis=0)
    wide = lambda value: value.astype(jnp.float32)
    blocks = []
    for m in range(2):
        m00 = mat_ref[m, :half, :half]
        m11 = mat_ref[m, half:, half:]
        u01 = mat_ref[m, :half, half:]
        l10 = mat_ref[m, half:, :half]
        u00, l00 = jnp.where(upper, m00, zero), jnp.where(upper, zero, m00)
        u11, l11 = jnp.where(upper, m11, zero), jnp.where(upper, zero, m11)
        blocks.append(
            (lanes(u00, u01, -l00), lanes(l00, u00, u01), lanes(u11, -l10, -l11), lanes(l10, l11, u11))
        )
    stacked = [tall(*pair) for pair in zip(*blocks)]
    singles, peaks = [], [None, None]
    for wave_ref, energy_ref in ((own_ref, e_own_ref), (other_ref, e_other_ref)):
        r0, r1 = wave_ref[0, :half], wave_ref[0, half:]
        i0, i1 = wave_ref[1, :half], wave_ref[1, half:]
        totals = [None, None]
        for left, right, times in zip(
            stacked,
            (tall(r0, r1, i0), tall(r0, i0, i1), tall(r1, i0, i1), tall(r0, r1, i1)),
            (r0, i0, r1, i1),
        ):
            image = dot(left, right)
            times = wide(times)
            for m in range(2):
                part = jnp.sum(image[m * half : (m + 1) * half] * times, axis=0)
                totals[m] = part if totals[m] is None else totals[m] + part
        energy = energy_ref[...]
        power, quad = 2.0 * totals[0][None], 2.0 * totals[1][None]
        single = (power / energy, energy / quad)
        singles.append(single)
        for m in range(2):
            top = jnp.max(single[m], axis=1, keepdims=True)
            peaks[m] = top if peaks[m] is None else jnp.maximum(peaks[m], top)
    part_of = role()
    lane = lax.broadcasted_iota(jnp.int32, (1, 128), 1)
    at = ((lax.axis_index("x") * 2 + core) * 2 + part_of) * 2
    mark = jnp.where(lane == at, peaks[0], jnp.where(lane == at + 1, peaks[1], -jnp.inf))
    n_f = out_ref.shape[0] // 4
    share = own_ref.shape[2] // n_f
    for f in range(n_f):
        own, other = (lanes(*(p[:, f * share : (f + 1) * share] for p in single)) for single in singles)
        for py in range(2):
            for pz in range(2):
                mine = jnp.where(core == 0, py, pz) == part_of
                out_ref[(py * 2 + pz) * n_f + f] = lanes(jnp.where(mine, own, other), mark)


def fan_kernel(near_ref, out_hbm, sems):
    bins = near_ref.shape[1]
    sends = [
        pltpu.make_async_copy(near_ref.at[:, to % bins], out_hbm.at[to], sems.at[to]) for to in range(out_hbm.shape[0])
    ]
    for copy in sends:
        copy.start()
    for copy in sends:
        copy.wait()


def fan(near, n_y):
    n_z, _, *rest = near.shape
    return pl.pallas_call(
        fan_kernel,
        out_shape=jax.ShapeDtypeStruct((n_y, n_z, *rest), near.dtype),
        in_specs=[pl.BlockSpec(memory_space=pltpu.VMEM)],
        out_specs=pl.BlockSpec(memory_space=pltpu.HBM),
        scratch_shapes=[pltpu.SemaphoreType.DMA((n_y,))],
        cost_estimate=pl.CostEstimate(flops=0, bytes_accessed=10 * near.size, transcendentals=0),
        compiler_params=pltpu.CompilerParams(vmem_limit_bytes=4 * MIB),
        name="fan",
    )(near)


def peaks_kernel(parts_ref, out_ref):
    width = out_ref.shape[2]
    top = parts_ref[0, :, width:]
    for source in range(1, parts_ref.shape[0]):
        top = jnp.maximum(top, parts_ref[source, :, width:])
    for to in range(out_ref.shape[0]):
        out_ref[to] = top


def total_kernel(count, parts_ref, tops_ref, first_ref, second_ref):
    odd_y, odd_z = lax.axis_index("yl") == 1, lax.axis_index("zl") == 1
    n_f = parts_ref.shape[0] // 4
    width = tops_ref.shape[2]
    share = width // 2
    top = tops_ref[0]
    for source in range(1, tops_ref.shape[0]):
        top = jnp.maximum(top, tops_ref[source])
    lane = lax.broadcasted_iota(jnp.int32, (1, width), 1)
    total = jnp.zeros((1, width), jnp.float32)
    for f in range(n_f):
        for part_of in range(2):
            low = part_of * 2 * n_f + f if f % 2 == 0 else part_of * n_f + f
            high = low + (n_f if f % 2 == 0 else 2 * n_f)
            odd = odd_z if f % 2 == 0 else odd_y
            part = jnp.where(odd, parts_ref[high, :, :width], parts_ref[low, :, :width])
            at = (f * 2 + part_of) * 2
            total += part / jnp.where(lane < share, top[:, at : at + 1], top[:, at + 1 : at + 2])
    total = total * (1.0 / count)
    first_ref[...] = total[:, :share]
    second_ref[...] = total[:, share:]


def kernel_call(kernel, outs, operands, scratch=(), limit=4 * MIB, flops=0, dtype=jnp.float32):
    vmem = pl.BlockSpec(memory_space=pltpu.VMEM)
    cost = pl.CostEstimate(flops=flops, bytes_accessed=sum(a.size for a in operands), transcendentals=0)
    return pl.pallas_call(
        kernel,
        out_shape=tuple(jax.ShapeDtypeStruct(s, dtype) for s in outs),
        in_specs=[vmem] * len(operands),
        out_specs=[vmem] * len(outs),
        scratch_shapes=list(scratch),
        cost_estimate=cost,
        compiler_params=pltpu.CompilerParams(vmem_limit_bytes=limit),
    )(*operands)


def body(shape, replicas, csm, inverse):
    n_y, n_z, n_x, n_c = shape
    bins, points, _, width = replicas.shape
    natural = Layout(major_to_minor=(0, 1, 2))
    rows, given = pack(n_z, csm, inverse, replicas)
    got = lax.ppermute(with_layout_constraint(given, natural), ALL, partners(shape))
    got = with_layout_constraint(got, natural)
    kept = lax.dynamic_index_in_dim(replicas, role(), 0, keepdims=False)

    near = lax.all_to_all(rows, ALL, 0, 0, axis_index_groups=lines(shape, True), tiled=True)
    both = lax.all_to_all(fan(near, n_y), ALL, 0, 0, axis_index_groups=lines(shape, False), tiled=True)

    waves, energies = [], []
    for held in (kept, got):
        waves.append(jnp.transpose(held, (1, 2, 0)))
        wide = held.astype(jnp.float32)
        energies.append((jnp.sum(wide * wide, axis=(1, 2)) + 1e-06)[None])
    n_f = n_x * n_c
    share = points // n_f
    (parts,) = kernel_call(
        forms_kernel,
        ((4 * n_f, 1, 2 * share + 128),),
        (both, *waves, *energies),
        scratch=[pltpu.VMEM((2, width, width), jnp.bfloat16)],
        limit=24 * MIB,
        flops=2 * 2 * 12 * 2 * (width // 2) ** 2 * points,
    )
    parts = lax.all_to_all(parts, ("yl", "zl", "x", "c"), 0, 0, tiled=True)
    (tops,) = kernel_call(peaks_kernel, ((n_y * n_z // 4, 1, 128),), (parts,))
    tops = lax.all_to_all(tops, ("yh", "zh"), 0, 0, tiled=True)
    total = functools.partial(total_kernel, bins * n_f)
    first, second = kernel_call(total, ((1, share), (1, share)), (parts, tops))
    return first[0], second[0]


def solution(mesh):
    side = round(mesh.shape["grid"] ** 0.5)
    shape = (side, side, mesh.shape["freq"] // 2, 2)
    fine = Mesh(mesh.devices.reshape(side // 2, 2, side // 2, 2, *shape[2:]), ALL)
    grid, freq = ALL[:4], ALL[4:]
    in_specs = (P(freq, grid, None, None), P(freq, None, grid, None), P(freq, None, grid, None))
    out_specs = (P(ALL), P(ALL))

    def run(*inputs):
        return body(shape, *inputs)

    return jax.shard_map(run, mesh=fine, in_specs=in_specs, out_specs=out_specs, check_vma=False)
```

profile of v0, /device:TPU:1, one launch (start us, length us, event | category | flops | bytes accessed | tf_op | source)
XLA Modules:
  0.0 98.3 jit_solution(3154596108736354264)
XLA Ops:
  0.6 2.2 %pack.1 = (bf16[8,2,2,8,512]{4,3,2,1,0:T(8,128)(2,1)}, bf16[512,2,512]{2,1,0:T(2,128)(2,1)}) custom-call(bf16[2,2,8,512]{3,2,1,0:T(8,128)(2,1)} %csm_hbm.1, bf16[2,2,8,512]{3,2,1,0:T(8,128)(2,1)} %inverse_hbm.1, bf16[2,512,2,512]{3,2,1,0:T(2,128)(2,1)} %held_hbm.1), custom_call_target="tpu_custom_call" | custom-call | bytes 2097152 | tf_op jit(solution)/shard_map/pack/pallas_call | solution.py:88
  2.9 0.0 copy-start
  2.9 17.1 %all_to_all.20.near_ref = bf16[8,2,2,8,512]{4,3,2,1,0:T(8,128)(2,1)S(1)} all-to-all(bf16[8,2,2,8,512]{4,3,2,1,0:T(8,128)(2,1)} %get-tuple-element.6), channel_id=1, replica_groups={{0,8,16,24,32,40,48,56},{2,10,18,26,34,42,50,58},{4,12,20,28,36,44,52,6..., dimensions={0} | all-to-all | bytes 524288 | tf_op jit(solution)/shard_map/all_to_all | solution.py:255
  20.0 1.1 %fan.1 = bf16[8,8,2,8,512]{4,3,2,1,0:T(8,128)(2,1)} custom-call(bf16[8,2,2,8,512]{4,3,2,1,0:T(8,128)(2,1)S(1)} %all_to_all.20.near_ref), custom_call_target="tpu_custom_call" | custom-call | bytes 1310720 | tf_op jit(solution)/shard_map/fan/pallas_call | solution.py:188
  21.1 10.0 %all-to-all-start.1 = ((bf16[8,8,2,8,512]{4,3,2,1,0:T(8,128)(2,1)}), bf16[8,8,2,8,512]{4,3,2,1,0:T(8,128)(2,1)S(1)}, u32[]{:S(2)}, u32[]{:S(2)}) async-start(bf16[8,8,2,8,512]{4,3,2,1,0:T(8,128)(2,1)} %fan.1), calls=%async_computation.1 | async-start | bytes 2097152 | tf_op jit(solution)/shard_map/all_to_all | solution.py:256
  31.1 3.4 %collective-permute-start = (bf16[512,2,512]{2,1,0:T(2,128)(2,1)}, bf16[512,2,512]{2,1,0:T(2,128)(2,1)}, u32[]{:S(2)}, u32[]{:S(2)}) collective-permute-start(bf16[512,2,512]{2,1,0:T(2,128)(2,1)} %get-tuple-element.7), channel_id=1, source_target_pairs={{0,64},{2,66},{4,68},{6,70},{8,72},{10,74},{12,76},{14,78},{16,80}... | collective-permute-start | bytes 3145736 | tf_op jit(solution)/shard_map/ppermute | solution.py:251
  34.5 0.0 copy-done
  34.5 1.7 %constant_dynamic-slice_fusion = bf16[1,512,2,512]{3,2,1,0:T(2,128)(2,1)} fusion(bf16[2,512,2,512]{3,2,1,0:T(2,128)(2,1)S(1)} %copy-done, s32[]{:T(128)S(6)} %select_n.9), kind=kLoop, calls=%fused_computation.4 | loop fusion | bytes 2097156 | tf_op jit(solution)/shard_map/jit(dynamic_index_in_dim)/dynamic_slice | solution.py:253
  36.2 2.4 %copy.5 = bf16[1,512,2,512]{1,3,2,0:T(8,128)(2,1)S(1)} copy(bf16[1,512,2,512]{3,2,1,0:T(2,128)(2,1)} %constant_dynamic-slice_fusion) | data formatting | bytes 2097152 | tf_op jit(solution)/shard_map/jit(dynamic_index_in_dim)/dynamic_slice | solution.py:253
  38.7 0.3 multiply_reduce_fusion.1
  39.0 17.7 %collective-permute-done = bf16[512,2,512]{2,1,0:T(2,128)(2,1)} collective-permute-done((bf16[512,2,512]{2,1,0:T(2,128)(2,1)}, bf16[512,2,512]{2,1,0:T(2,128)(2,1)}, u32[]{:S(2)}, u32[]{:S(2)}) %collective-permute-start) | collective-permute-done | bytes 1048608 | tf_op jit(solution)/shard_map/ppermute | solution.py:251
  56.6 2.4 %copy.6 = bf16[512,2,512]{0,2,1:T(8,128)(2,1)S(1)} copy(bf16[512,2,512]{2,1,0:T(2,128)(2,1)} %collective-permute-done) | data formatting | bytes 2097152 | tf_op jit(solution)/shard_map/layout_constraint | solution.py:252
  59.1 2.9 %multiply_reduce_fusion = f32[512]{0:T(512)S(1)} fusion(bf16[512,2,512]{2,1,0:T(2,128)(2,1)} %collective-permute-done), kind=kLoop, calls=%fused_computation | loop fusion | flops 1572352 | bytes 1050624 | tf_op jit(solution)/shard_map/reduce_sum | solution.py:262
  62.0 0.0 all-to-all-done.1.rows_ref
  62.0 3.6 %shard_map.50 = f32[32,1,256]{2,1,0:T(1,128)S(1)} custom-call(bf16[8,8,2,8,512]{4,3,2,1,0:T(8,128)(2,1)S(1)} %all-to-all-done.1.rows_ref, bf16[2,512,512]{2,1,0:T(8,128)(2,1)S(1)} %bitcast.9, bf16[2,512,512]{2,1,0:T(8,128)(2,1)S(1)} %bitcast.10, f32[1,512]{1,0:T(1,128)S(1)} %bitcast.11, f32[1,512]{1,0:T(1,128)S(1)} %bitcast.12), custom_call_target="tpu_custom_call" | custom-call | flops 3221225472 | bytes 1573888 | tf_op jit(solution)/shard_map/pallas_call | solution.py:235
  65.6 14.2 %all_to_all.21.parts_ref = f32[32,1,256]{2,1,0:T(1,128)S(1)} all-to-all(f32[32,1,256]{2,1,0:T(1,128)S(1)} %shard_map.50), channel_id=1, replica_groups=mesh['yh'=4,'yl'=2,'zh'=4,'zl'=2,'x'=4,'c'=2] {'yl','zl','x','c'}, dimensions={0} | all-to-all | bytes 65536 | tf_op jit(solution)/shard_map/all_to_all | solution.py:273
  79.9 17.8 %all_to_all.22.tops_ref = f32[16,1,128]{2,1,0:T(1,128)S(1)} all-to-all(f32[16,1,128]{2,1,0:T(1,128)S(1)} %shard_map.51), channel_id=1, replica_groups=mesh['yh'=4,'yl'=2,'zh'=4,'zl'=2,'x'=4,'c'=2] {'yh','zh'}, dimensions={0} | all-to-all | bytes 16384 | tf_op jit(solution)/shard_map/all_to_all | solution.py:275
  97.6 0.7 shard_map.52
  (3 shorter events, 0.1 us)
Async XLA Ops:
  2.9 31.7 %copy-start = (bf16[2,512,2,512]{3,2,1,0:T(2,128)(2,1)S(1)}, bf16[2,512,2,512]{3,2,1,0:T(2,128)(2,1)}, u32[]{:S(2)}) copy-start(bf16[2,512,2,512]{3,2,1,0:T(2,128)(2,1)} %held_hbm.1) | copy-start | bytes 6291460
  21.1 40.9 %all-to-all-start.1 = ((bf16[8,8,2,8,512]{4,3,2,1,0:T(8,128)(2,1)}), bf16[8,8,2,8,512]{4,3,2,1,0:T(8,128)(2,1)S(1)}, u32[]{:S(2)}, u32[]{:S(2)}) async-start(bf16[8,8,2,8,512]{4,3,2,1,0:T(8,128)(2,1)} %fan.1), calls=%async_computation.1 | async-start | bytes 2097152 | tf_op jit(solution)/shard_map/all_to_all | solution.py:256
  31.1 25.5 %collective-permute-start = (bf16[512,2,512]{2,1,0:T(2,128)(2,1)}, bf16[512,2,512]{2,1,0:T(2,128)(2,1)}, u32[]{:S(2)}, u32[]{:S(2)}) collective-permute-start(bf16[512,2,512]{2,1,0:T(2,128)(2,1)} %get-tuple-element.7), channel_id=1, source_target_pairs={{0,64},{2,66},{4,68},{6,70},{8,72},{10,74},{12,76},{14,78},{16,80}... | collective-permute-start | bytes 3145736 | tf_op jit(solution)/shard_map/ppermute | solution.py:251
where the time goes:
time: 98.8 us; the launch traced here: 98.3 us
  blocking collectives  49.1 us (50%)
  waiting for transfers between devices  17.7 us (18%)
  starting transfers between devices  13.4 us (14%)
  Pallas kernels  7.68 us (8%)
  local copies, waits for them, and re-layouts  6.6 us (7%)
  other arithmetic  3.21 us (3%)
    all_to_all x1, blocking collectives, body(): tops = lax.all_to_all(tops, ('yh', 'zh'), 0, 0, tiled=True)  17.8 us
    ppermute x1, waiting for transfers between devices, body(): lax.ppermute(with_layout_constraint(given, natural), ALL, partners(shape))  17.7 us
    all_to_all x1, blocking collectives, body(): lax.all_to_all(rows, ALL, 0, 0, axis_index_groups=lines(shape, True), til...  17.1 us
    all_to_all x1, blocking collectives, body(): parts = lax.all_to_all(parts, ('yl', 'zl', 'x', 'c'), 0, 0, tiled=True)  14.2 us
    all_to_all x1, starting transfers between devices, body(): lax.all_to_all(fan(near, n_y), ALL, 0, 0, axis_index_groups=lines(shape,...  10 us
    pallas_call x3, Pallas kernels, kernel_call(): pl.pallas_call(kernel, out_shape=tuple((jax.ShapeDtypeStruct(s, dtype) fo...  4.35 us
    dynamic_slice x2, local copies, waits for them, and re-layouts, body(): kept = lax.dynamic_index_in_dim(replicas, role(), 0, keepdims=False)  4.15 us
    ppermute x1, starting transfers between devices, body(): lax.ppermute(with_layout_constraint(given, natural), ALL, partners(shape))  3.36 us
  transfers between devices with their start and end apart: 2, of which 1 were waited for; matrix products, arithmetic and copies ran while one was open for 10% of the time, Pallas kernels for 0%

commit v1 on v0

--- a/solution.py
+++ b/solution.py
@@ -32,13 +32,13 @@
     pairs = []
     for core in range(shape[3]):
         plane = ids[..., core]
-        other = plane[np.arange(shape[0]) ^ 1] if core == 0 else plane[:, np.arange(shape[1]) ^ 1]
+        other = plane[:, np.arange(shape[1]) ^ 1] if core == 0 else plane[np.arange(shape[0]) ^ 1]
         pairs += zip(plane.ravel().tolist(), other.ravel().tolist())
     return pairs
 
 
 def role():
-    return jnp.where(lax.axis_index("c") == 0, lax.axis_index("yl"), lax.axis_index("zl"))
+    return jnp.where(lax.axis_index("c") == 0, lax.axis_index("zl"), lax.axis_index("yl"))
 
 
 def pack_kernel(n_z, csm_hbm, inverse_hbm, held_hbm, rows_hbm, given_hbm, matrices, packed, room, sems):
@@ -56,7 +56,7 @@
         pltpu.make_async_copy(room.at[k], given_hbm.at[pl.ds(k * size, size)], sems.at[at + k]) for k in range(parts)
     ]
     at += parts
-    sends = [pltpu.make_async_copy(packed, rows_hbm.at[to], sems.at[at + to]) for to in range(to_all)]
+    sends = [pltpu.make_async_copy(packed.at[to % bins], rows_hbm.at[to], sems.at[at + to]) for to in range(to_all)]
     for copy in reads + takes:
         copy.start()
     y = lax.axis_index("yh") * 2 + lax.axis_index("yl")
@@ -88,7 +88,7 @@
     return pl.pallas_call(
         functools.partial(pack_kernel, n_z),
         out_shape=(
-            jax.ShapeDtypeStruct((n_z, bins, 2, depth, width), csm.dtype),
+            jax.ShapeDtypeStruct((n_z, 2, depth, width), csm.dtype),
             jax.ShapeDtypeStruct(held.shape[1:], held.dtype),
         ),
         in_specs=[hbm] * 3,
@@ -168,15 +168,12 @@
         own, other = (lanes(*(p[:, f * share : (f + 1) * share] for p in single)) for single in singles)
         for py in range(2):
             for pz in range(2):
-                mine = jnp.where(core == 0, py, pz) == part_of
+                mine = jnp.where(core == 0, pz, py) == part_of
                 out_ref[(py * 2 + pz) * n_f + f] = lanes(jnp.where(mine, own, other), mark)
 
 
 def fan_kernel(near_ref, out_hbm, sems):
-    bins = near_ref.shape[1]
-    sends = [
-        pltpu.make_async_copy(near_ref.at[:, to % bins], out_hbm.at[to], sems.at[to]) for to in range(out_hbm.shape[0])
-    ]
+    sends = [pltpu.make_async_copy(near_ref, out_hbm.at[to], sems.at[to]) for to in range(out_hbm.shape[0])]
     for copy in sends:
         copy.start()
     for copy in sends:
@@ -184,10 +181,9 @@
 
 
 def fan(near, n_y):
-    n_z, _, *rest = near.shape
     return pl.pallas_call(
         fan_kernel,
-        out_shape=jax.ShapeDtypeStruct((n_y, n_z, *rest), near.dtype),
+        out_shape=jax.ShapeDtypeStruct((n_y, *near.shape), near.dtype),
         in_specs=[pl.BlockSpec(memory_space=pltpu.VMEM)],
         out_specs=pl.BlockSpec(memory_space=pltpu.HBM),
         scratch_shapes=[pltpu.SemaphoreType.DMA((n_y,))],
@@ -218,9 +214,9 @@
     total = jnp.zeros((1, width), jnp.float32)
     for f in range(n_f):
         for part_of in range(2):
-            low = part_of * 2 * n_f + f if f % 2 == 0 else part_of * n_f + f
-            high = low + (n_f if f % 2 == 0 else 2 * n_f)
-            odd = odd_z if f % 2 == 0 else odd_y
+            low = part_of * n_f + f if f % 2 == 0 else part_of * 2 * n_f + f
+            high = low + (2 * n_f if f % 2 == 0 else n_f)
+            odd = odd_y if f % 2 == 0 else odd_z
             part = jnp.where(odd, parts_ref[high, :, :width], parts_ref[low, :, :width])
             at = (f * 2 + part_of) * 2
             total += part / jnp.where(lane < share, top[:, at : at + 1], top[:, at + 1 : at + 2])

time: 98.8 us -> 96.7 us (0.979)
  blocking collectives: 49.1 us -> 45.4 us
  waiting for transfers between devices: 17.7 us -> 20.4 us
  starting transfers between devices: 13.4 us -> 12.2 us
    ppermute x1, waiting for transfers between devices: 17.7 us -> 20.4 us  [body(): lax.ppermute(with_layout_constraint(given, natural), ALL, partners(shape))]
    all_to_all x1, blocking collectives: 14.2 us -> 12 us  [body(): parts = lax.all_to_all(parts, ('yl', 'zl', 'x', 'c'), 0, 0, tiled=True)]
    all_to_all x1, blocking collectives: 17.1 us -> 15.7 us  [body(): lax.all_to_all(rows, ALL, 0, 0, axis_index_groups=lines(shape, True), til...]
    ppermute x1, starting transfers between devices: 3.36 us -> 2.18 us  [body(): lax.ppermute(with_layout_constraint(given, natural), ALL, partners(shape))]
where the time goes in v1:
time: 96.7 us; the launch traced here: 96.2 us
  blocking collectives  45.4 us (47%)
  waiting for transfers between devices  20.4 us (21%)
  starting transfers between devices  12.2 us (13%)
  Pallas kernels  7.61 us (8%)
  local copies, waits for them, and re-layouts  6.6 us (7%)
  other arithmetic  3.21 us (3%)
    ppermute x1, waiting for transfers between devices, body(): lax.ppermute(with_layout_constraint(given, natural), ALL, partners(shape))  20.4 us
    all_to_all x1, blocking collectives, body(): tops = lax.all_to_all(tops, ('yh', 'zh'), 0, 0, tiled=True)  17.7 us
    all_to_all x1, blocking collectives, body(): lax.all_to_all(rows, ALL, 0, 0, axis_index_groups=lines(shape, True), til...  15.7 us
    all_to_all x1, blocking collectives, body(): parts = lax.all_to_all(parts, ('yl', 'zl', 'x', 'c'), 0, 0, tiled=True)  12 us
    all_to_all x1, starting transfers between devices, body(): lax.all_to_all(fan(near, n_y), ALL, 0, 0, axis_index_groups=lines(shape,...  10 us
    pallas_call x3, Pallas kernels, kernel_call(): pl.pallas_call(kernel, out_shape=tuple((jax.ShapeDtypeStruct(s, dtype) fo...  4.35 us
    dynamic_slice x2, local copies, waits for them, and re-layouts, body(): kept = lax.dynamic_index_in_dim(replicas, role(), 0, keepdims=False)  4.15 us
    reduce_sum x2, other arithmetic, body(): energies.append((jnp.sum(wide * wide, axis=(1, 2)) + 1e-06)[None])  3.19 us
  transfers between devices with their start and end apart: 2, of which 1 were waited for; matrix products, arithmetic and copies ran while one was open for 10% of the time, Pallas kernels for 0%

profile of v1, /device:TPU:1, one launch (start us, length us, event | category | flops | bytes accessed | tf_op | source)
XLA Modules:
  0.0 96.2 jit_solution(15221466398611372316)
XLA Ops:
  0.6 2.2 %pack.1 = (bf16[8,2,8,512]{3,2,1,0:T(8,128)(2,1)}, bf16[512,2,512]{2,1,0:T(2,128)(2,1)}) custom-call(bf16[2,2,8,512]{3,2,1,0:T(8,128)(2,1)} %csm_hbm.1, bf16[2,2,8,512]{3,2,1,0:T(8,128)(2,1)} %inverse_hbm.1, bf16[2,512,2,512]{3,2,1,0:T(2,128)(2,1)} %held_hbm.1), custom_call_target="tpu_custom_call" | custom-call | bytes 2097152 | tf_op jit(solution)/shard_map/pack/pallas_call | solution.py:88
  2.8 0.0 copy-start
  2.8 15.7 %all_to_all.20.near_ref = bf16[8,2,8,512]{3,2,1,0:T(8,128)(2,1)S(1)} all-to-all(bf16[8,2,8,512]{3,2,1,0:T(8,128)(2,1)} %get-tuple-element.6), channel_id=1, replica_groups={{0,8,16,24,32,40,48,56},{2,10,18,26,34,42,50,58},{4,12,20,28,36,44,52,6..., dimensions={0} | all-to-all | bytes 262144 | tf_op jit(solution)/shard_map/all_to_all | solution.py:251
  18.5 1.1 %fan.1 = bf16[8,8,2,8,512]{4,3,2,1,0:T(8,128)(2,1)} custom-call(bf16[8,2,8,512]{3,2,1,0:T(8,128)(2,1)S(1)} %all_to_all.20.near_ref), custom_call_target="tpu_custom_call" | custom-call | bytes 655360 | tf_op jit(solution)/shard_map/fan/pallas_call | solution.py:184
  19.6 10.0 %all-to-all-start.1 = ((bf16[8,8,2,8,512]{4,3,2,1,0:T(8,128)(2,1)}), bf16[8,8,2,8,512]{4,3,2,1,0:T(8,128)(2,1)S(1)}, u32[]{:S(2)}, u32[]{:S(2)}) async-start(bf16[8,8,2,8,512]{4,3,2,1,0:T(8,128)(2,1)} %fan.1), calls=%async_computation.1 | async-start | bytes 2097152 | tf_op jit(solution)/shard_map/all_to_all | solution.py:252
  29.7 2.2 %collective-permute-start = (bf16[512,2,512]{2,1,0:T(2,128)(2,1)}, bf16[512,2,512]{2,1,0:T(2,128)(2,1)}, u32[]{:S(2)}, u32[]{:S(2)}) collective-permute-start(bf16[512,2,512]{2,1,0:T(2,128)(2,1)} %get-tuple-element.7), channel_id=1, source_target_pairs={{0,8},{2,10},{4,12},{6,14},{8,0},{10,2},{12,4},{14,6},{16,24},{18,... | collective-permute-start | bytes 3145736 | tf_op jit(solution)/shard_map/ppermute | solution.py:247
  31.9 0.0 copy-done
  31.9 1.7 %constant_dynamic-slice_fusion = bf16[1,512,2,512]{3,2,1,0:T(2,128)(2,1)} fusion(bf16[2,512,2,512]{3,2,1,0:T(2,128)(2,1)S(1)} %copy-done, s32[]{:T(128)S(6)} %select_n.9), kind=kLoop, calls=%fused_computation.4 | loop fusion | bytes 2097156 | tf_op jit(solution)/shard_map/jit(dynamic_index_in_dim)/dynamic_slice | solution.py:249
  33.6 2.4 %copy.5 = bf16[1,512,2,512]{1,3,2,0:T(8,128)(2,1)S(1)} copy(bf16[1,512,2,512]{3,2,1,0:T(2,128)(2,1)} %constant_dynamic-slice_fusion) | data formatting | bytes 2097152 | tf_op jit(solution)/shard_map/jit(dynamic_index_in_dim)/dynamic_slice | solution.py:249
  36.1 0.3 multiply_reduce_fusion.1
  36.3 20.4 %collective-permute-done = bf16[512,2,512]{2,1,0:T(2,128)(2,1)} collective-permute-done((bf16[512,2,512]{2,1,0:T(2,128)(2,1)}, bf16[512,2,512]{2,1,0:T(2,128)(2,1)}, u32[]{:S(2)}, u32[]{:S(2)}) %collective-permute-start) | collective-permute-done | bytes 1048608 | tf_op jit(solution)/shard_map/ppermute | solution.py:247
  56.8 2.4 %copy.6 = bf16[512,2,512]{0,2,1:T(8,128)(2,1)S(1)} copy(bf16[512,2,512]{2,1,0:T(2,128)(2,1)} %collective-permute-done) | data formatting | bytes 2097152 | tf_op jit(solution)/shard_map/layout_constraint | solution.py:248
  59.2 2.9 %multiply_reduce_fusion = f32[512]{0:T(512)S(1)} fusion(bf16[512,2,512]{2,1,0:T(2,128)(2,1)} %collective-permute-done), kind=kLoop, calls=%fused_computation | loop fusion | flops 1572352 | bytes 1050624 | tf_op jit(solution)/shard_map/reduce_sum | solution.py:258
  62.1 0.0 all-to-all-done.1.rows_ref
  62.2 3.6 %shard_map.50 = f32[32,1,256]{2,1,0:T(1,128)S(1)} custom-call(bf16[8,8,2,8,512]{4,3,2,1,0:T(8,128)(2,1)S(1)} %all-to-all-done.1.rows_ref, bf16[2,512,512]{2,1,0:T(8,128)(2,1)S(1)} %bitcast.9, bf16[2,512,512]{2,1,0:T(8,128)(2,1)S(1)} %bitcast.10, f32[1,512]{1,0:T(1,128)S(1)} %bitcast.11, f32[1,512]{1,0:T(1,128)S(1)} %bitcast.12), custom_call_target="tpu_custom_call" | custom-call | flops 3221225472 | bytes 1573888 | tf_op jit(solution)/shard_map/pallas_call | solution.py:231
  65.7 12.0 %all_to_all.21.parts_ref = f32[32,1,256]{2,1,0:T(1,128)S(1)} all-to-all(f32[32,1,256]{2,1,0:T(1,128)S(1)} %shard_map.50), channel_id=1, replica_groups=mesh['yh'=4,'yl'=2,'zh'=4,'zl'=2,'x'=4,'c'=2] {'yl','zl','x','c'}, dimensions={0} | all-to-all | bytes 65536 | tf_op jit(solution)/shard_map/all_to_all | solution.py:269
  77.8 17.7 %all_to_all.22.tops_ref = f32[16,1,128]{2,1,0:T(1,128)S(1)} all-to-all(f32[16,1,128]{2,1,0:T(1,128)S(1)} %shard_map.51), channel_id=1, replica_groups=mesh['yh'=4,'yl'=2,'zh'=4,'zl'=2,'x'=4,'c'=2] {'yh','zh'}, dimensions={0} | all-to-all | bytes 16384 | tf_op jit(solution)/shard_map/all_to_all | solution.py:271
  95.5 0.7 shard_map.52
  (3 shorter events, 0.1 us)
Async XLA Ops:
  2.8 29.1 %copy-start = (bf16[2,512,2,512]{3,2,1,0:T(2,128)(2,1)S(1)}, bf16[2,512,2,512]{3,2,1,0:T(2,128)(2,1)}, u32[]{:S(2)}) copy-start(bf16[2,512,2,512]{3,2,1,0:T(2,128)(2,1)} %held_hbm.1) | copy-start | bytes 6291460
  19.6 42.5 %all-to-all-start.1 = ((bf16[8,8,2,8,512]{4,3,2,1,0:T(8,128)(2,1)}), bf16[8,8,2,8,512]{4,3,2,1,0:T(8,128)(2,1)S(1)}, u32[]{:S(2)}, u32[]{:S(2)}) async-start(bf16[8,8,2,8,512]{4,3,2,1,0:T(8,128)(2,1)} %fan.1), calls=%async_computation.1 | async-start | bytes 2097152 | tf_op jit(solution)/shard_map/all_to_all | solution.py:252
  29.7 27.1 %collective-permute-start = (bf16[512,2,512]{2,1,0:T(2,128)(2,1)}, bf16[512,2,512]{2,1,0:T(2,128)(2,1)}, u32[]{:S(2)}, u32[]{:S(2)}) collective-permute-start(bf16[512,2,512]{2,1,0:T(2,128)(2,1)} %get-tuple-element.7), channel_id=1, source_target_pairs={{0,8},{2,10},{4,12},{6,14},{8,0},{10,2},{12,4},{14,6},{16,24},{18,... | collective-permute-start | bytes 3145736 | tf_op jit(solution)/shard_map/ppermute | solution.py:247

commit v2 on v0

--- a/solution.py
+++ b/solution.py
@@ -41,23 +41,12 @@
     return jnp.where(lax.axis_index("c") == 0, lax.axis_index("yl"), lax.axis_index("zl"))
 
 
-def pack_kernel(n_z, csm_hbm, inverse_hbm, held_hbm, rows_hbm, given_hbm, matrices, packed, room, sems):
+def pack_kernel(n_z, csm_hbm, inverse_hbm, rows_hbm, matrices, packed, sems):
     bins, _, depth, width = csm_hbm.shape
-    to_all, (parts, size) = rows_hbm.shape[0], room.shape[:2]
-    chosen = 1 - role()
+    to_all = rows_hbm.shape[0]
     reads = [pltpu.make_async_copy(ref, matrices.at[k], sems.at[k]) for k, ref in enumerate((csm_hbm, inverse_hbm))]
-    at = len(reads)
-    takes = [
-        pltpu.make_async_copy(held_hbm.at[chosen, pl.ds(k * size, size)], room.at[k], sems.at[at + k])
-        for k in range(parts)
-    ]
-    at += parts
-    gives = [
-        pltpu.make_async_copy(room.at[k], given_hbm.at[pl.ds(k * size, size)], sems.at[at + k]) for k in range(parts)
-    ]
-    at += parts
-    sends = [pltpu.make_async_copy(packed, rows_hbm.at[to], sems.at[at + to]) for to in range(to_all)]
-    for copy in reads + takes:
+    sends = [pltpu.make_async_copy(packed, rows_hbm.at[to], sems.at[2 + to]) for to in range(to_all)]
+    for copy in reads:
         copy.start()
     y = lax.axis_index("yh") * 2 + lax.axis_index("yl")
     z = lax.axis_index("zh") * 2 + lax.axis_index("zl")
@@ -72,37 +61,63 @@
             real = matrices[m, b, 0].astype(jnp.float32) * weight
             imag = matrices[m, b, 1].astype(jnp.float32)
             packed[b, m] = jnp.where(col >= row, real, imag).astype(packed.dtype)
-    for take, give in zip(takes, gives):
-        take.wait()
-        give.start()
     for copy in sends:
         copy.start()
-    for copy in sends + gives:
+    for copy in sends:
         copy.wait()
 
 
-def pack(n_z, csm, inverse, held, parts=4):
+def pack(n_z, csm, inverse):
     bins, _, depth, width = csm.shape
-    _, points, two, _ = held.shape
     hbm = pl.BlockSpec(memory_space=pltpu.HBM)
     return pl.pallas_call(
         functools.partial(pack_kernel, n_z),
-        out_shape=(
-            jax.ShapeDtypeStruct((n_z, bins, 2, depth, width), csm.dtype),
-            jax.ShapeDtypeStruct(held.shape[1:], held.dtype),
-        ),
-        in_specs=[hbm] * 3,
-        out_specs=[hbm] * 2,
+        out_shape=jax.ShapeDtypeStruct((n_z, bins, 2, depth, width), csm.dtype),
+        in_specs=[hbm] * 2,
+        out_specs=hbm,
         scratch_shapes=[
             pltpu.VMEM((2, *csm.shape), csm.dtype),
             pltpu.VMEM((bins, 2, depth, width), csm.dtype),
+            pltpu.SemaphoreType.DMA((2 + n_z,)),
+        ],
+        cost_estimate=pl.CostEstimate(flops=0, bytes_accessed=10 * csm.size, transcendentals=0),
+        compiler_params=pltpu.CompilerParams(vmem_limit_bytes=61 * MIB),
+        name="pack",
+    )(csm, inverse)
+
+
+def pick_kernel(flip, held_ref, out_ref, room, arrived, left):
+    chosen = 1 - role() if flip else role()
+    parts, size = room.shape[0], room.shape[1]
+    reads = [
+        pltpu.make_async_copy(held_ref.at[chosen, pl.ds(k * size, size)], room.at[k], arrived.at[k])
+        for k in range(parts)
+    ]
+    writes = [pltpu.make_async_copy(room.at[k], out_ref.at[pl.ds(k * size, size)], left.at[k]) for k in range(parts)]
+    for read in reads:
+        read.start()
+    for read, write in zip(reads, writes):
+        read.wait()
+        write.start()
+    for write in writes:
+        write.wait()
+
+
+def pick(flip, held, parts=4):
+    _, points, two, width = held.shape
+    return pl.pallas_call(
+        functools.partial(pick_kernel, flip),
+        out_shape=jax.ShapeDtypeStruct(held.shape[1:], held.dtype),
+        in_specs=[pl.BlockSpec(memory_space=pltpu.HBM)],
+        out_specs=pl.BlockSpec(memory_space=pltpu.HBM),
+        scratch_shapes=[
             pltpu.VMEM((parts, points // parts, two, width), held.dtype),
-            pltpu.SemaphoreType.DMA((2 + 2 * parts + n_z,)),
+            pltpu.SemaphoreType.DMA((parts,)),
+            pltpu.SemaphoreType.DMA((parts,)),
         ],
         cost_estimate=pl.CostEstimate(flops=0, bytes_accessed=2 * held.size, transcendentals=0),
         compiler_params=pltpu.CompilerParams(vmem_limit_bytes=61 * MIB),
-        name="pack",
-    )(csm, inverse, held)
+    )(held)
 
 
 def forms_kernel(rows_ref, own_ref, other_ref, e_own_ref, e_other_ref, out_ref, mat_ref):
@@ -247,7 +262,8 @@
     n_y, n_z, n_x, n_c = shape
     bins, points, _, width = replicas.shape
     natural = Layout(major_to_minor=(0, 1, 2))
-    rows, given = pack(n_z, csm, inverse, replicas)
+    rows = pack(n_z, csm, inverse)
+    given = pick(True, replicas)
     got = lax.ppermute(with_layout_constraint(given, natural), ALL, partners(shape))
     got = with_layout_constraint(got, natural)
     kept = lax.dynamic_index_in_dim(replicas, role(), 0, keepdims=False)

time: 98.8 us -> 98.1 us (level)
  waiting for transfers between devices: 17.7 us -> 16.3 us
  Pallas kernels: 7.68 us -> 9.02 us
    pallas_call x1 -> x2, Pallas kernels: 2.23 us -> 3.62 us  [the longest x1 2.05 us: pick(): pl.pallas_call(functools.partial(pick_kernel, flip), out_shape=jax.ShapeD...]
    ppermute x1, waiting for transfers between devices: 17.7 us -> 16.3 us  [body(): lax.ppermute(with_layout_constraint(given, natural), ALL, partners(shape))]
  transfers between devices with their start and end apart: 2 -> 2, of which waited for: 1 -> 1; matrix products, arithmetic and copies ran while one was open for 10% -> 9% of each run, Pallas kernels for 0% -> 2%
where the time goes in v2:
time: 98.1 us; the launch traced here: 97.5 us
  blocking collectives  48.9 us (50%)
  waiting for transfers between devices  16.3 us (17%)
  starting transfers between devices  13.4 us (14%)
  Pallas kernels  9.02 us (9%)
  local copies, waits for them, and re-layouts  5.85 us (6%)
  other arithmetic  3.21 us (3%)
    all_to_all x1, blocking collectives, body(): tops = lax.all_to_all(tops, ('yh', 'zh'), 0, 0, tiled=True)  17.8 us
    all_to_all x1, blocking collectives, body(): lax.all_to_all(rows, ALL, 0, 0, axis_index_groups=lines(shape, True), til...  17 us
    ppermute x1, waiting for transfers between devices, body(): lax.ppermute(with_layout_constraint(given, natural), ALL, partners(shape))  16.3 us
    all_to_all x1, blocking collectives, body(): parts = lax.all_to_all(parts, ('yl', 'zl', 'x', 'c'), 0, 0, tiled=True)  14.2 us
    all_to_all x1, starting transfers between devices, body(): lax.all_to_all(fan(near, n_y), ALL, 0, 0, axis_index_groups=lines(shape,...  10 us
    pallas_call x3, Pallas kernels, kernel_call(): pl.pallas_call(kernel, out_shape=tuple((jax.ShapeDtypeStruct(s, dtype) fo...  4.35 us
    dynamic_slice x2, local copies, waits for them, and re-layouts, body(): kept = lax.dynamic_index_in_dim(replicas, role(), 0, keepdims=False)  3.4 us
    ppermute x1, starting transfers between devices, body(): lax.ppermute(with_layout_constraint(given, natural), ALL, partners(shape))  3.37 us
  transfers between devices with their start and end apart: 2, of which 1 were waited for; matrix products, arithmetic and copies ran while one was open for 9% of the time, Pallas kernels for 2%

profile of v2, /device:TPU:1, one launch (start us, length us, event | category | flops | bytes accessed | tf_op | source)
XLA Modules:
  0.0 97.5 jit_solution(1793045375993912343)
XLA Ops:
  0.6 1.6 %pack.1 = bf16[8,2,2,8,512]{4,3,2,1,0:T(8,128)(2,1)} custom-call(bf16[2,2,8,512]{3,2,1,0:T(8,128)(2,1)} %csm_hbm.1, bf16[2,2,8,512]{3,2,1,0:T(8,128)(2,1)} %inverse_hbm.1), custom_call_target="tpu_custom_call" | custom-call | bytes 163840 | tf_op jit(solution)/shard_map/pack/pallas_call | solution.py:73
  2.2 17.0 %all_to_all.20.near_ref = bf16[8,2,2,8,512]{4,3,2,1,0:T(8,128)(2,1)S(1)} all-to-all(bf16[8,2,2,8,512]{4,3,2,1,0:T(8,128)(2,1)} %pack.1), channel_id=1, replica_groups={{0,8,16,24,32,40,48,56},{2,10,18,26,34,42,50,58},{4,12,20,28,36,44,52,6..., dimensions={0} | all-to-all | bytes 524288 | tf_op jit(solution)/shard_map/all_to_all | solution.py:271
  19.2 1.1 %fan.1 = bf16[8,8,2,8,512]{4,3,2,1,0:T(8,128)(2,1)} custom-call(bf16[8,2,2,8,512]{4,3,2,1,0:T(8,128)(2,1)S(1)} %all_to_all.20.near_ref), custom_call_target="tpu_custom_call" | custom-call | bytes 1310720 | tf_op jit(solution)/shard_map/fan/pallas_call | solution.py:203
  20.3 10.0 %all-to-all-start.1 = ((bf16[8,8,2,8,512]{4,3,2,1,0:T(8,128)(2,1)}), bf16[8,8,2,8,512]{4,3,2,1,0:T(8,128)(2,1)S(1)}, u32[]{:S(2)}, u32[]{:S(2)}) async-start(bf16[8,8,2,8,512]{4,3,2,1,0:T(8,128)(2,1)} %fan.1), calls=%async_computation.1 | async-start | bytes 2097152 | tf_op jit(solution)/shard_map/all_to_all | solution.py:272
  30.3 2.1 %shard_map.50 = bf16[512,2,512]{2,1,0:T(2,128)(2,1)} custom-call(bf16[2,512,2,512]{3,2,1,0:T(2,128)(2,1)} %held_ref.1), custom_call_target="tpu_custom_call" | custom-call | bytes 2097152 | tf_op jit(solution)/shard_map/pallas_call | solution.py:108
  32.4 3.4 %collective-permute-start = (bf16[512,2,512]{2,1,0:T(2,128)(2,1)}, bf16[512,2,512]{2,1,0:T(2,128)(2,1)}, u32[]{:S(2)}, u32[]{:S(2)}) collective-permute-start(bf16[512,2,512]{2,1,0:T(2,128)(2,1)} %shard_map.50), channel_id=1, source_target_pairs={{0,64},{2,66},{4,68},{6,70},{8,72},{10,74},{12,76},{14,78},{16,80}... | collective-permute-start | bytes 3145736 | tf_op jit(solution)/shard_map/ppermute | solution.py:267
  35.7 1.9 %constant_dynamic-slice_fusion = bf16[1,512,2,512]{3,2,1,0:T(2,128)(2,1)S(1)} fusion(bf16[2,512,2,512]{3,2,1,0:T(2,128)(2,1)} %held_ref.1, s32[]{:T(128)S(6)} %select_n.9), kind=kLoop, calls=%fused_computation.4 | loop fusion | bytes 2097156 | tf_op jit(solution)/shard_map/jit(dynamic_index_in_dim)/dynamic_slice | solution.py:269
  37.7 1.5 %copy.5 = bf16[1,512,2,512]{1,3,2,0:T(8,128)(2,1)S(1)} copy(bf16[1,512,2,512]{3,2,1,0:T(2,128)(2,1)S(1)} %constant_dynamic-slice_fusion) | data formatting | bytes 2097152 | tf_op jit(solution)/shard_map/jit(dynamic_index_in_dim)/dynamic_slice | solution.py:269
  39.2 0.3 multiply_reduce_fusion.1
  39.4 16.3 %collective-permute-done = bf16[512,2,512]{2,1,0:T(2,128)(2,1)} collective-permute-done((bf16[512,2,512]{2,1,0:T(2,128)(2,1)}, bf16[512,2,512]{2,1,0:T(2,128)(2,1)}, u32[]{:S(2)}, u32[]{:S(2)}) %collective-permute-start) | collective-permute-done | bytes 1048608 | tf_op jit(solution)/shard_map/ppermute | solution.py:267
  55.8 2.4 %copy.6 = bf16[512,2,512]{0,2,1:T(8,128)(2,1)S(1)} copy(bf16[512,2,512]{2,1,0:T(2,128)(2,1)} %collective-permute-done) | data formatting | bytes 2097152 | tf_op jit(solution)/shard_map/layout_constraint | solution.py:268
  58.2 2.9 %multiply_reduce_fusion = f32[512]{0:T(512)S(1)} fusion(bf16[512,2,512]{2,1,0:T(2,128)(2,1)} %collective-permute-done), kind=kLoop, calls=%fused_computation | loop fusion | flops 1572352 | bytes 1050624 | tf_op jit(solution)/shard_map/reduce_sum | solution.py:278
  61.2 0.0 all-to-all-done.1.rows_ref
  61.2 3.6 %shard_map.51 = f32[32,1,256]{2,1,0:T(1,128)S(1)} custom-call(bf16[8,8,2,8,512]{4,3,2,1,0:T(8,128)(2,1)S(1)} %all-to-all-done.1.rows_ref, bf16[2,512,512]{2,1,0:T(8,128)(2,1)S(1)} %bitcast.9, bf16[2,512,512]{2,1,0:T(8,128)(2,1)S(1)} %bitcast.10, f32[1,512]{1,0:T(1,128)S(1)} %bitcast.11, f32[1,512]{1,0:T(1,128)S(1)} %bitcast.12), custom_call_target="tpu_custom_call" | custom-call | flops 3221225472 | bytes 1573888 | tf_op jit(solution)/shard_map/pallas_call | solution.py:250
  64.8 14.2 %all_to_all.21.parts_ref = f32[32,1,256]{2,1,0:T(1,128)S(1)} all-to-all(f32[32,1,256]{2,1,0:T(1,128)S(1)} %shard_map.51), channel_id=1, replica_groups=mesh['yh'=4,'yl'=2,'zh'=4,'zl'=2,'x'=4,'c'=2] {'yl','zl','x','c'}, dimensions={0} | all-to-all | bytes 65536 | tf_op jit(solution)/shard_map/all_to_all | solution.py:289
  79.0 17.8 %all_to_all.22.tops_ref = f32[16,1,128]{2,1,0:T(1,128)S(1)} all-to-all(f32[16,1,128]{2,1,0:T(1,128)S(1)} %shard_map.52), channel_id=1, replica_groups=mesh['yh'=4,'yl'=2,'zh'=4,'zl'=2,'x'=4,'c'=2] {'yh','zh'}, dimensions={0} | all-to-all | bytes 16384 | tf_op jit(solution)/shard_map/all_to_all | solution.py:291
  96.8 0.7 shard_map.53
  (3 shorter events, 0.1 us)
Async XLA Ops:
  20.3 40.9 %all-to-all-start.1 = ((bf16[8,8,2,8,512]{4,3,2,1,0:T(8,128)(2,1)}), bf16[8,8,2,8,512]{4,3,2,1,0:T(8,128)(2,1)S(1)}, u32[]{:S(2)}, u32[]{:S(2)}) async-start(bf16[8,8,2,8,512]{4,3,2,1,0:T(8,128)(2,1)} %fan.1), calls=%async_computation.1 | async-start | bytes 2097152 | tf_op jit(solution)/shard_map/all_to_all | solution.py:272
  32.4 23.4 %collective-permute-start = (bf16[512,2,512]{2,1,0:T(2,128)(2,1)}, bf16[512,2,512]{2,1,0:T(2,128)(2,1)}, u32[]{:S(2)}, u32[]{:S(2)}) collective-permute-start(bf16[512,2,512]{2,1,0:T(2,128)(2,1)} %shard_map.50), channel_id=1, source_target_pairs={{0,64},{2,66},{4,68},{6,70},{8,72},{10,74},{12,76},{14,78},{16,80}... | collective-permute-start | bytes 3145736 | tf_op jit(solution)/shard_map/ppermute | solution.py:267
